TPU v7x, 32 devices: a whole 2x2x4 slice. The times are simulated.
32 devices in a mesh: dp: 8 (over z, x), tensor: 4 (over y, core).
Axes of the slice: x: 2, y: 2, z: 4, core: 2. Of those that a mesh axis runs over, the one named last changes fastest.
Arguments:
- layer_input: bfloat16 [8192, 2048], P('dp'), may hold values from -6 to 6
- ln1_gain: bfloat16 [2048], replicated, may hold values from 0.099609375 to 1.8984375
- ln1_bias: bfloat16 [2048], replicated, may hold values from -3 to 3
- ln2_gain: bfloat16 [2048], replicated, may hold values from 0.099609375 to 1.8984375
- ln2_bias: bfloat16 [2048], replicated, may hold values from -3 to 3
- qkv_weight: bfloat16 [2048, 6144], P(None, 'tensor'), may hold values from -0.125 to 0.125
- qkv_bias: bfloat16 [6144], P('tensor'), may hold values from -1.75 to 1.75
- dense_weight: bfloat16 [2048, 2048], P(None, 'tensor'), may hold values from -0.75 to 0.75
- dense_bias: bfloat16 [2048], replicated, may hold values from -3 to 3
- fc1_weight: bfloat16 [2048, 8192], P(None, 'tensor'), may hold values from -0.125 to 0.125
- fc1_bias: bfloat16 [8192], P('tensor'), may hold values from -3 to 3
- fc2_weight: bfloat16 [2048, 8192], P(None, 'tensor'), may hold values from -0.0625 to 0.0625
- fc2_bias: bfloat16 [2048], replicated, may hold values from -3 to 3
- cotangent: bfloat16 [8192, 2048], P('dp'), may hold values from -6 to 6
Outputs:
- output: bfloat16 [8192, 2048], P('dp')
- input_grad: bfloat16 [8192, 2048], P('dp')
- grad_ln1_gain: float32 [2048], replicated
- grad_ln1_bias: float32 [2048], replicated
- grad_ln2_gain: float32 [2048], replicated
- grad_ln2_bias: float32 [2048], replicated
- grad_qkv_weight: float32 [2048, 6144], P('dp', 'tensor')
- grad_qkv_bias: float32 [6144], P('tensor')
- grad_dense_weight: float32 [2048, 2048], P('dp', 'tensor')
- grad_dense_bias: float32 [2048], replicated
- grad_fc1_weight: float32 [2048, 8192], P('dp', 'tensor')
- grad_fc1_bias: float32 [8192], P('tensor')
- grad_fc2_weight: float32 [2048, 8192], P('dp', 'tensor')
- grad_fc2_bias: float32 [2048], replicated
All inputs are finite; a program needn't handle non-finite values.
Results may differ from a plain program's by a relative error of at most 0.013.
Values may be sent and summed in bfloat16 or wider, within the bound.
A program may use at most 256 MiB of HBM per device.

v0:
```python
import itertools
import math
from functools import partial

import jax
import jax.numpy as jnp
from jax import lax
from jax.experimental import pallas as pl
from jax.experimental.pallas import tpu as pltpu
from jax.sharding import PartitionSpec as P

HEADS = 8
SEQ = 1024
HEAD_DIM = 256
ROT = 64
EPSILON = 1e-05
VMEM_LIMIT = 63 * 1024 * 1024

f32 = jnp.float32
bf16 = jnp.bfloat16
NN = (((1,), (0,)), ((), ()))
NT = (((1,), (1,)), ((), ()))
TN = (((0,), (0,)), ((), ()))


def dot(a, b, dims=NN):
    return lax.dot_general(a, b, dims, preferred_element_type=f32)


def turn(block, cos_table, sine_table):
    half_rot = ROT // 2
    head = block[:, :128]
    lane = lax.broadcasted_iota(jnp.int32, head.shape, 1)
    other = jnp.where(lane < half_rot, pltpu.roll(head, 128 - half_rot, 1), pltpu.roll(head, half_rot, 1))
    return jnp.concatenate([head * cos_table + other * sine_table, block[:, 128:]], 1)


def angle_tables():
    half_rot = ROT // 2
    lane = jnp.arange(128)
    frequency = jnp.exp((lane % half_rot).astype(f32) * (-2.0 * math.log(10000.0) / ROT))
    frequency = jnp.where(lane < ROT, frequency, 0.0)
    step = jnp.arange(32, dtype=f32)
    angles = jnp.concatenate([step, 32.0 * step])[:, None] * frequency[None, :]
    cos, sin = jnp.cos(angles), jnp.sin(angles)
    sign = jnp.where(lane < half_rot, -1.0, 1.0)[None, :]
    return jnp.concatenate([cos[:32], sin[:32], cos[32:], sin[32:], jnp.broadcast_to(sign, (8, 128))], 0)


CHUNK = 512
MESH = pl.DeviceIdType.MESH
VEC_ROWS = 8
VECTORS = 8
NORM_ROWS = 128


class Slots:
    def __init__(self, count):
        self.free = [(n, []) for n in range(count)]

    def take(self):
        slot, waits = self.free.pop(0)
        for wait in waits:
            wait()
        return slot

    def give(self, slot, *waits):
        self.free.append((slot, list(waits)))

    def drain(self):
        for _, waits in self.free:
            for wait in waits:
                wait()


def layer_kernel(
    x_hbm, c_hbm, table_in, fc1_hbm, fc2_hbm, wqkv_hbm, dense_hbm, *refs,
    jobs, orders, heads, block=256,
):
    vec_hbm, refs = refs[:VECTORS], refs[VECTORS:]
    (
        out_hbm, grad_hbm, keep_hbm, last_hbm, small_out, r1_hbm, r2_hbm, core_hbm, y_hbm,
        attn_in, mlp_in, cot, act, hg, qg, ctx, mean_ref, rstd_ref, cos_ref, sin_ref, vec, raw, w1buf, w2buf,
        s1, s2, s3, k2, ld1, ldm, ld2, piece, xrow, small, small_in,
        load_sem, send_sem, recv_sem, keep_sem,
    ) = refs
    rows, width = cot.shape
    hidden = act.shape[1]
    nb = width // 8
    quarter = rows // 4
    me, own = lax.axis_index("dp"), lax.axis_index("tensor")
    dp_bits = [lax.rem(lax.div(me, 1 << k), 2) for k in range(3)]
    t_bits = [lax.rem(lax.div(own, 1 << k), 2) for k in range(2)]

    def dp_flip(*bits):
        return me + sum((1 - 2 * dp_bits[k]) * (1 << k) for k in bits)

    def t_flip(*bits):
        return own + sum((1 - 2 * t_bits[k]) * (1 << k) for k in bits)

    def dp_partner(bit):
        return (dp_flip(bit), own)

    def t_partner(bit):
        return (me, t_flip(bit))

    partners = [dp_partner(k) for k in range(3)] + [t_partner(k) for k in range(2)]
    barrier = pltpu.get_barrier_semaphore()
    for partner in partners:
        pl.semaphore_signal(barrier, inc=1, device_id=partner, device_id_type=MESH)

    copies = itertools.count()

    def send_copy(src, dst, partner):
        n = next(copies)
        copy = pltpu.make_async_remote_copy(
            src_ref=src, dst_ref=dst, send_sem=send_sem.at[n], recv_sem=recv_sem.at[n], device_id=partner, device_id_type=MESH
        )
        copy.start()
        return copy

    loads = itertools.count()

    def load(src, dst):
        copy = pltpu.make_async_copy(src, dst, load_sem.at[next(loads)])
        copy.start()
        return copy

    load_x = load(x_hbm, act)
    load_v = [load(v, raw.at[n, pl.ds(0, v.shape[0])]) for n, v in enumerate(vec_hbm)]

    def mlp_weights(j):
        slot = j % 2
        at = pl.ds(j * CHUNK, CHUNK)
        return [load(fc1_hbm.at[:, at], w1buf.at[slot]), load(fc2_hbm.at[:, at], w2buf.at[slot])]

    def head_weights(h):
        slot = h % 2
        base = 3 * h * HEAD_DIM
        return [
            load(wqkv_hbm.at[:, pl.ds(base, 2 * HEAD_DIM)], w1buf.at[slot]),
            load(wqkv_hbm.at[:, pl.ds(base + 2 * HEAD_DIM, HEAD_DIM)], w2buf.at[slot, :, pl.ds(0, HEAD_DIM)]),
            load(dense_hbm.at[:, pl.ds(h * HEAD_DIM, HEAD_DIM)], w2buf.at[slot, :, pl.ds(HEAD_DIM, HEAD_DIM)]),
        ]

    weights = {("mlp", 0): mlp_weights(0)}
    load_c = load(c_hbm, cot)
    weights["mlp", 1] = mlp_weights(1)
    tiles = hidden // CHUNK

    small[...] = jnp.zeros_like(small)
    for copy in load_v:
        copy.wait()
    for n in range(VECTORS):
        packed = raw[n].astype(f32)
        if n == 6:
            packed = packed + raw[5].astype(f32)
        for i in range(vec_hbm[n].shape[0]):
            vec[n : n + 1, i * 128 : (i + 1) * 128] = packed[i : i + 1, :]
    low_cos, low_sin = table_in[0:32, :], table_in[32:64, :]
    sign = table_in[128:129, :]
    for n in range(SEQ // 32):
        high_cos, high_sin = table_in[64 + n : 65 + n, :], table_in[96 + n : 97 + n, :]
        cos_ref[n * 32 : (n + 1) * 32, :] = high_cos * low_cos - high_sin * low_sin
        sin_ref[n * 32 : (n + 1) * 32, :] = sign * (high_sin * low_cos + high_cos * low_sin)

    load_x.wait()

    def norm_rows(i, _):
        part = pl.ds(pl.multiple_of(i * NORM_ROWS, NORM_ROWS), NORM_ROWS)
        x = act[part, :].astype(f32)
        mean = jnp.mean(x, -1, keepdims=True)
        centred = x - mean
        rstd = lax.rsqrt(jnp.mean(centred * centred, -1, keepdims=True) + EPSILON)
        u = centred * rstd
        attn_in[part, :] = (u * vec[0:1, :] + vec[1:2, :]).astype(bf16)
        mlp_in[part, :] = (u * vec[2:3, :] + vec[3:4, :]).astype(bf16)
        mean_ref[part, :] = mean
        rstd_ref[part, :] = rstd
        return 0

    lax.fori_loop(0, rows // NORM_ROWS, norm_rows, 0)
    load_c.wait()
    pl.semaphore_wait(barrier, len(partners))

    s1_slots, s2_slots, s3_slots, k2_slots = Slots(s1.shape[0]), Slots(s2.shape[0]), Slots(s3.shape[0]), Slots(k2.shape[0])
    state = {}

    def operands(c):
        n_fc = hidden // CHUNK
        n_qkv = qg.shape[1] // CHUNK
        if c < n_fc:
            return cot, act, c
        if c < 2 * n_fc:
            return mlp_in, hg, c - n_fc
        if c < 2 * n_fc + n_qkv:
            return attn_in, qg, c - 2 * n_fc
        return cot, ctx, c - 2 * n_fc - n_qkv

    def block_of(lhs, index):
        return lhs[:, pl.ds(pl.multiple_of(index * nb, nb), nb)]

    def w1(c):
        lhs, rhs, j = operands(c)
        one, two, three = orders[c]
        slot = s1_slots.take()
        base = dp_flip(one, two, three)

        def body(n, _):
            second, third = n // 2, lax.rem(n, 2)
            index = base - second * (1 - 2 * dp_bits[two]) * (1 << two) - third * (1 - 2 * dp_bits[three]) * (1 << three)
            s1[slot, n] = dot(block_of(lhs, index), rhs[:, j * CHUNK : (j + 1) * CHUNK], TN).astype(bf16)
            return 0

        lax.fori_loop(0, 4, body, 0)
        copy = send_copy(s1.at[slot], r1_hbm.at[c], dp_partner(one))
        s1_slots.give(slot, copy.wait_send)
        state[c] = copy

    def w2(c):
        lhs, rhs, j = operands(c)
        one, two, three = orders[c]
        state[c].wait_recv()
        loaded = load(r1_hbm.at[c], ld1)
        slot, kept = s2_slots.take(), k2_slots.take()
        loaded.wait()

        def part(base, n, out):
            def body(i, _):
                index = base - i * (1 - 2 * dp_bits[three]) * (1 << three)
                out[i] = (dot(block_of(lhs, index), rhs[:, j * CHUNK : (j + 1) * CHUNK], TN) + ld1[n + i].astype(f32)).astype(bf16)
                return 0

            lax.fori_loop(0, 2, body, 0)

        part(dp_flip(two, three), 0, s2.at[slot])
        copy = send_copy(s2.at[slot], r2_hbm.at[c], dp_partner(two))
        s2_slots.give(slot, copy.wait_send)
        part(dp_flip(three), 2, k2.at[kept])
        state[c] = (copy, kept)

    def a3(c):
        copy, kept = state[c]
        three = orders[c][2]
        copy.wait_recv()
        loaded = load(r2_hbm.at[c], ld2)
        slot = s3_slots.take()
        loaded.wait()
        s3[slot] = (k2[kept, 0].astype(f32) + ld2[0].astype(f32)).astype(bf16)
        columns = pl.ds(c * CHUNK, CHUNK)
        copy = send_copy(s3.at[slot], last_hbm.at[:, columns], dp_partner(three))
        s3_slots.give(slot, copy.wait_send)
        k2[kept, 1] = (k2[kept, 1].astype(f32) + ld2[1].astype(f32)).astype(bf16)
        keep = pltpu.make_async_copy(k2.at[kept, 1], keep_hbm.at[:, columns], keep_sem.at[c])
        keep.start()
        k2_slots.give(kept, keep.wait)
        state[c] = copy

    def mlp(j):
        slot = j % 2
        for copy in weights.pop(("mlp", j)):
            copy.wait()
        at = j * CHUNK
        bias = vec[4:5, at : at + CHUNK]

        def body(i, sums):
            part = pl.ds(pl.multiple_of(i * block, block), block)
            h = dot(mlp_in[part, :], w1buf[slot]) + bias
            above = dot(cot[part, :], w2buf[slot])
            cdf = 0.5 + 0.5 * lax.erf(h * (2.0**-0.5))
            density = jnp.exp(h * h * -0.5) * ((2.0 * math.pi) ** -0.5)
            act[part, at : at + CHUNK] = (h * cdf).astype(bf16)
            low = (above * (cdf + h * density)).astype(bf16)
            hg[part, at : at + CHUNK] = low
            above_sum = jnp.sum(cot[part, at : at + CHUNK].astype(f32), 0, keepdims=True)
            return sums[0] + jnp.sum(low.astype(f32), 0, keepdims=True), sums[1] + above_sum

        zero = jnp.zeros((1, CHUNK), f32)
        bias_sum, above_sum = lax.fori_loop(0, rows // block, body, (zero, zero))
        small[4:5, at : at + CHUNK] = bias_sum
        small[6:7, at : at + CHUNK] = above_sum
        if j + 2 < tiles:
            weights["mlp", j + 2] = mlp_weights(j + 2)
        else:
            h = j + 2 - tiles
            weights["head", h] = head_weights(h)

    def attention(n):
        if n > 0:
            return
        for h in range(heads):
            for copy in weights.pop(("head", h)):
                copy.wait()
        lax.fori_loop(0, heads, one_head, 0)

    def one_head(slot, _):
        base = pl.multiple_of(3 * HEAD_DIM * slot, HEAD_DIM)
        scale = HEAD_DIM ** (-0.5)

        def third(n):
            return pl.ds(pl.multiple_of(base + n * HEAD_DIM, HEAD_DIM), HEAD_DIM)

        mine = pl.ds(pl.multiple_of(slot * HEAD_DIM, HEAD_DIM), HEAD_DIM)

        def scoped(qkv_ref, g_ref, dk_ref, dv_ref):
            def project(i, _):
                part = pl.ds(pl.multiple_of(i * block, block), block)
                acc = dot(attn_in[part, :], w1buf[slot]) + vec[7:8, pl.ds(base, 2 * HEAD_DIM)]
                cos, sin = cos_ref[part, :], sin_ref[part, :]
                for n in range(2):
                    at = n * HEAD_DIM
                    qkv_ref[part, at : at + HEAD_DIM] = turn(acc[:, at : at + HEAD_DIM], cos, sin).astype(bf16)
                acc = dot(attn_in[part, :], w2buf[slot, :, 0:HEAD_DIM]) + vec[7:8, third(2)]
                qkv_ref[part, 2 * HEAD_DIM :] = acc.astype(bf16)
                g_ref[part, :] = dot(cot[part, :], w2buf[slot, :, HEAD_DIM : 2 * HEAD_DIM]).astype(bf16)
                return 0

            lax.fori_loop(0, rows // block, project, 0)
            for i in reversed(range(SEQ // block)):
                part = pl.ds(i * block, block)
                key_end = (i + 1) * block
                keys = pl.ds(0, key_end)
                q, g = qkv_ref[part, 0:HEAD_DIM], g_ref[part, :]
                k, v = qkv_ref[keys, HEAD_DIM : 2 * HEAD_DIM], qkv_ref[keys, 2 * HEAD_DIM :]
                scores = dot(q, k, NT) * scale
                row_id = i * block + lax.broadcasted_iota(jnp.int32, scores.shape, 0)
                col_id = lax.broadcasted_iota(jnp.int32, scores.shape, 1)
                scores = jnp.where(col_id <= row_id, scores, -1e30)
                e = jnp.exp(scores - jnp.max(scores, -1, keepdims=True))
                probs = e / jnp.sum(e, -1, keepdims=True)
                low = probs.astype(bf16)
                ctx[part, mine] = dot(low, v).astype(bf16)
                prob_grad = dot(g, v, NT)
                delta = jnp.sum(probs * prob_grad, -1, keepdims=True)
                score_grad = (probs * (prob_grad - delta)).astype(bf16)
                dv = dot(low, g, TN)
                dk = dot(score_grad, q, TN)
                if i == SEQ // block - 1:
                    dv_ref[...] = dv
                    dk_ref[...] = dk
                else:
                    dv_ref[keys, :] += dv
                    dk_ref[keys, :] += dk
                dq = (dot(score_grad, k) * scale).astype(bf16).astype(f32)
                qg[part, third(0)] = turn(dq, cos_ref[part, :], -sin_ref[part, :]).astype(bf16)
            dk = (dk_ref[...] * scale).astype(bf16).astype(f32)
            qg[:, third(1)] = turn(dk, cos_ref[...], -sin_ref[...]).astype(bf16)
            qg[:, third(2)] = dv_ref[...].astype(bf16)
            for n in range(3):
                small[5:6, third(n)] = jnp.sum(qg[:, third(n)].astype(f32), 0, keepdims=True)

        pl.run_scoped(
            scoped,
            pltpu.VMEM((SEQ, 3 * HEAD_DIM), bf16),
            pltpu.VMEM((SEQ, HEAD_DIM), bf16),
            pltpu.VMEM((SEQ, HEAD_DIM), f32),
            pltpu.VMEM((SEQ, HEAD_DIM), f32),
        )
        return 0

    def quarter_of(n):
        index = own + (1 - n // 2) * (1 - 2 * t_bits[0]) + (1 - lax.rem(n, 2)) * (1 - 2 * t_bits[1]) * 2
        return pl.ds(pl.multiple_of(index * quarter, quarter), quarter)

    def back_tiles(buf, first_hbm, first, second_hbm, second, x_tiles, store):
        step = CHUNK // 2

        def scoped(first_w, second_w, x_w, sems):
            def copies_of(d, slot):
                at = pl.ds(pl.multiple_of(d * step, step), step)
                made = [
                    pltpu.make_async_copy(first_hbm.at[at, :], first_w.at[slot], sems.at[slot, 0]),
                    pltpu.make_async_copy(second_hbm.at[at, :], second_w.at[slot], sems.at[slot, 1]),
                ]
                if x_tiles:
                    made.append(pltpu.make_async_copy(x_hbm.at[:, at], x_w.at[slot], sems.at[slot, 2]))
                return made

            n_steps = width // step
            for copy in copies_of(0, 0):
                copy.start()

            def body(e, _):
                for half in range(2):
                    d = 2 * e + half
                    for copy in copies_of(d, half):
                        copy.wait()

                    @pl.when(d + 1 < n_steps)
                    def _():
                        for copy in copies_of(d + 1, 1 - half):
                            copy.start()

                    columns = pl.ds(half * step, step)

                    def one(m, sums):
                        for n in (2 * m, 2 * m + 1):
                            part = quarter_of(n)
                            a = dot(first[part, :], first_w[half], NT)
                            b = dot(second[part, :], second_w[half], NT)
                            at = pl.ds(pl.multiple_of(e * 2 * quarter + lax.rem(n, 2) * quarter, quarter), quarter)
                            buf[m, at, columns], terms = store(d, part, a, b, x_w.at[half])
                            sums = tuple(s + t for s, t in zip(sums, terms))
                        return sums

                    count = 4 if x_tiles else 0
                    sums = lax.fori_loop(0, 2, one, tuple(jnp.zeros((1, step), f32) for _ in range(count)))
                    if x_tiles:
                        at = pl.ds(pl.multiple_of(d * step, step), step)
                        small[0:4, at] = jnp.concatenate(sums, 0)
                return 0

            lax.fori_loop(0, n_steps // 2, body, 0)

        pl.run_scoped(
            scoped,
            pltpu.VMEM((2, step, first.shape[1]), bf16),
            pltpu.VMEM((2, step, second.shape[1]), bf16),
            pltpu.VMEM((2, rows if x_tiles else 16, step), bf16),
            pltpu.SemaphoreType.DMA((2, 3)),
        )

    def input_tiles():
        step = CHUNK // 2

        def store(d, part, a, b, x_tile):
            at = pl.ds(pl.multiple_of(d * step, step), step)
            u = (x_tile[part, :].astype(f32) - mean_ref[part, :]) * rstd_ref[part, :]
            terms = [jnp.sum(t, 0, keepdims=True) for t in (a * u, a, b * u, b)]
            return (a * vec[0:1, at] + b * vec[2:3, at]).astype(bf16), terms

        back_tiles(w1buf, wqkv_hbm, qg, fc1_hbm, hg, True, store)

    def output_tiles():
        back_tiles(w2buf, dense_hbm, ctx, fc2_hbm, act, False, lambda d, part, a, b, x_tile: ((a + b).astype(bf16), []))

    e_tiles = width // CHUNK
    buffers = (w1buf, w2buf)
    results = (grad_hbm, out_hbm)

    def sum_start(k):
        (input_tiles, output_tiles)[k]()
        state["sum", k] = send_copy(buffers[k].at[0], core_hbm.at[k], t_partner(0))

    def half_of(k, half, dst):
        return [
            load(core_hbm.at[k, pl.ds(e * 2 * quarter + half * quarter, quarter), :], dst.at[e]) for e in range(e_tiles)
        ]

    def sum_middle(k):
        first = state["sum", k]
        first.wait_recv()
        loaded = half_of(k, 0, ld1)
        slot = s1_slots.take()
        for copy in loaded:
            copy.wait()
        for e in range(e_tiles):
            s1[slot, e] = (buffers[k][1, pl.ds(e * 2 * quarter, quarter), :].astype(f32) + ld1[e].astype(f32)).astype(bf16)
        copy = send_copy(s1.at[slot], y_hbm.at[k], t_partner(1))
        s1_slots.give(slot, copy.wait_send)
        first.wait_send()
        state["sum", k] = copy

    own_rows = pl.ds(pl.multiple_of(own * quarter, quarter), quarter)

    def rows_of(index):
        return pl.ds(pl.multiple_of(index * quarter, quarter), quarter)

    def sum_late(k):
        x_load = load(x_hbm.at[own_rows, :], xrow)
        half_loads = half_of(k, 1, ld1)
        state["sum", k].wait_recv()
        y_load = load(y_hbm.at[k], ldm)
        for copy in half_loads + [x_load, y_load]:
            copy.wait()
        totals = [
            buffers[k][1, pl.ds(e * 2 * quarter + quarter, quarter), :].astype(f32) + ld1[e].astype(f32) + ldm[e].astype(f32)
            for e in range(e_tiles)
        ]
        parts = [(e * CHUNK, (e + 1) * CHUNK) for e in range(e_tiles)]
        if k == 0:
            mean, rstd = mean_ref[own_rows, :], rstd_ref[own_rows, :]
            us = [(xrow[:, a:b].astype(f32) - mean) * rstd for a, b in parts]
            mean_w = sum(jnp.sum(t, -1, keepdims=True) for t in totals) * (1.0 / width)
            mean_wu = sum(jnp.sum(t * u, -1, keepdims=True) for t, u in zip(totals, us)) * (1.0 / width)
            for (a, b), t, u in zip(parts, totals, us):
                piece[k, :, a:b] = (cot[own_rows, a:b].astype(f32) + rstd * (t - mean_w - u * mean_wu)).astype(bf16)
        else:
            for (a, b), t in zip(parts, totals):
                piece[k, :, a:b] = (xrow[:, a:b].astype(f32) + t + vec[6:7, a:b]).astype(bf16)
        result = results[k]
        state["pieces", k] = [
            load(piece.at[k], result.at[own_rows, :]),
            send_copy(piece.at[k], result.at[own_rows, :], t_partner(1)),
            send_copy(piece.at[k], result.at[own_rows, :], t_partner(0)),
        ]

    def sum_gather(k):
        result = results[k]
        state["pieces", k][1].wait_recv()
        at = rows_of(t_flip(1))
        state["pieces", k].append(send_copy(result.at[at, :], result.at[at, :], t_partner(0)))

    def small_round(n):
        if n > 0:
            copy = state["small"]
            copy.wait()
            if n <= 2:
                small[0:4, :] += small_in[n - 1, 0:4, :]
            else:
                small[...] += small_in[n - 1]
        if n < 5:
            partner = t_partner(n) if n < 2 else dp_partner(n - 2)
            state["small"] = send_copy(small, small_in.at[n], partner)
        else:
            state["small"] = load(small, small_out)

    actions = dict(
        m=mlp, h=attention, a=w1, b=w2, c=a3, i=lambda k: sum_start(k), j=sum_middle, k=sum_late, l=sum_gather, s=small_round
    )
    for kind, n in jobs:
        actions[kind](n)

    for c in range(len(orders)):
        state[c].wait_recv()
    for k in range(2):
        local, first, second, third = state["pieces", k]
        local.wait()
        first.wait_send()
        second.wait()
        third.wait()
        state["sum", k]
    for slots in (s1_slots, s2_slots, s3_slots, k2_slots):
        slots.drain()
    state["small"].wait()


ORDER = " ".join(
    [
        "m0 a4 a0 m1",
        "m2 a5 m3 a7",
        "a2 h0 b4 h1",
        "b7 a1 a10 b5",
        "c4 i0 c7 a11",
        "s0 s1 b2 j0",
        "a8 c5 b1 s2",
        "i1 c2 j1 a3",
        "b11 a6 b10 c1",
        "b8 k1 c11 b3",
        "c8 c3 s3 b6",
        "a9 c10 l1 s4",
        "b0 s5 k0 c6",
        "b9 c0 c9 l0",
    ]
).split()
Z_FIRST = (0, 5, 10)


def layer_call(x, c, vectors, fc1, fc2, qkv_weight, dense):
    rows, width = x.shape
    hidden, qkv_columns, context_columns = fc1.shape[1], qkv_weight.shape[1], dense.shape[1]
    heads = qkv_columns // (3 * HEAD_DIM)
    total = 2 * hidden + qkv_columns + context_columns
    chunks = total // CHUNK
    vectors = [v.reshape(-1, 128) for v in vectors]
    jobs = [(word[0], int(word[1:])) for word in ORDER]
    orders = [(1, 0, 2) if n in Z_FIRST else (0, 1, 2) for n in range(chunks)]
    quarter, nb = rows // 4, width // 8
    anywhere = pl.BlockSpec(memory_space=pl.ANY)
    local = pl.BlockSpec(memory_space=pltpu.VMEM)
    shape = jax.ShapeDtypeStruct
    outs = [
        shape((rows, width), bf16),
        shape((rows, width), bf16),
        shape((nb, total), bf16),
        shape((nb, total), bf16),
        shape((8, width), f32),
        shape((chunks, 4, nb, CHUNK), bf16),
        shape((chunks, 2, nb, CHUNK), bf16),
        shape((2, width // CHUNK * 2 * quarter, CHUNK), bf16),
        shape((2, width // CHUNK, quarter, CHUNK), bf16),
    ]
    vmem = pltpu.VMEM
    scratch = [
        vmem((rows, width), bf16),
        vmem((rows, width), bf16),
        vmem((rows, width), bf16),
        vmem((rows, hidden), bf16),
        vmem((rows, hidden), bf16),
        vmem((rows, qkv_columns), bf16),
        vmem((rows, context_columns), bf16),
        vmem((rows, 1), f32),
        vmem((rows, 1), f32),
        vmem((SEQ, 128), f32),
        vmem((SEQ, 128), f32),
        vmem((VEC_ROWS, width), f32),
        vmem((VECTORS, width // 128, 128), bf16),
        vmem((2, width, CHUNK), bf16),
        vmem((2, width, CHUNK), bf16),
        vmem((5, 4, nb, CHUNK), bf16),
        vmem((6, 2, nb, CHUNK), bf16),
        vmem((6, nb, CHUNK), bf16),
        vmem((6, 2, nb, CHUNK), bf16),
        vmem((4, nb, CHUNK), bf16),
        vmem((4, nb, CHUNK), bf16),
        vmem((2, nb, CHUNK), bf16),
        vmem((2, quarter, width), bf16),
        vmem((quarter, width), bf16),
        vmem((8, width), f32),
        vmem((5, 8, width), f32),
        pltpu.SemaphoreType.DMA((88,)),
        pltpu.SemaphoreType.DMA((56,)),
        pltpu.SemaphoreType.DMA((56,)),
        pltpu.SemaphoreType.DMA((chunks,)),
    ]
    flops = 6 * rows * width * (2 * hidden + qkv_columns + context_columns)
    return pl.pallas_call(
        partial(layer_kernel, jobs=jobs, orders=orders, heads=heads),
        in_specs=[anywhere, anywhere, local] + [anywhere] * (4 + VECTORS),
        out_specs=[anywhere] * len(outs),
        out_shape=outs,
        scratch_shapes=scratch,
        compiler_params=pltpu.CompilerParams(vmem_limit_bytes=VMEM_LIMIT, collective_id=0, has_side_effects=True),
        cost_estimate=pl.CostEstimate(flops=flops, bytes_accessed=1 << 27, transcendentals=2 * rows * hidden),
        name="layer",
    )(x, c, angle_tables(), fc1, fc2, qkv_weight, dense, *vectors)


def finish_kernel(kept_ref, last_ref, out_ref, grad_ref, *refs):
    at = 0
    for ref in refs[:-2]:
        columns = slice(at, at + ref.shape[1])
        ref[...] = kept_ref[:, columns].astype(f32) + last_ref[:, columns].astype(f32)
        at += ref.shape[1]
    refs[-2][...] = out_ref[...]
    refs[-1][...] = grad_ref[...]


def finish_call(kept, last, output, input_grad, sizes, steps=4):
    nb, total = kept.shape
    rows, width = output.shape

    def tiles(count, columns):
        return pl.BlockSpec((count // steps, columns), lambda i: (i, 0))

    ins = [tiles(nb, total), tiles(nb, total), tiles(rows, width), tiles(rows, width)]
    outs = [tiles(nb, n) for n in sizes] + [tiles(rows, width)] * 2
    return pl.pallas_call(
        finish_kernel,
        grid=(steps,),
        in_specs=ins,
        out_specs=outs,
        out_shape=[jax.ShapeDtypeStruct((nb, n), f32) for n in sizes] + [jax.ShapeDtypeStruct((rows, width), bf16)] * 2,
        cost_estimate=pl.CostEstimate(flops=nb * total, bytes_accessed=8 * (nb * total + rows * width), transcendentals=0),
        name="finish",
    )(kept, last, output, input_grad)


def fused(
    layer_input,
    ln1_gain,
    ln1_bias,
    ln2_gain,
    ln2_bias,
    qkv_weight,
    qkv_bias,
    dense_weight,
    dense_bias,
    fc1_weight,
    fc1_bias,
    fc2_weight,
    fc2_bias,
    cotangent,
):
    whole_out, whole_grad, kept, last, small, *_ = layer_call(
        layer_input,
        cotangent,
        (ln1_gain, ln1_bias, ln2_gain, ln2_bias, fc1_bias, dense_bias, fc2_bias, qkv_bias),
        fc1_weight,
        fc2_weight,
        qkv_weight,
        dense_weight,
    )
    hidden, qkv_columns = fc1_weight.shape[1], qkv_weight.shape[1]
    grad_fc2, grad_fc1, grad_qkv, grad_dense, output, input_grad = finish_call(
        kept, last, whole_out, whole_grad, (hidden, hidden, qkv_columns, dense_weight.shape[1])
    )
    return (
        output,
        input_grad,
        small[0],
        small[1],
        small[2],
        small[3],
        grad_qkv,
        small[5, :qkv_columns],
        grad_dense,
        small[6],
        grad_fc1,
        small[4, :hidden],
        grad_fc2,
        small[6],
    )


def fits(mesh):
    return mesh.shape["dp"] == 8 and mesh.shape["tensor"] == 4


def normalize(x_float, gain_row, shift_row):
    row_mean = jnp.mean(x_float, -1, keepdims=True)
    centred = x_float - row_mean
    spread = jnp.mean(centred * centred, -1, keepdims=True)
    return centred * lax.rsqrt(spread + EPSILON) * gain_row + shift_row


def rotary_tables():
    half_rot = ROT // 2
    freq_index = jnp.arange(half_rot, dtype=jnp.float32)
    frequency = jnp.exp(freq_index * (-2.0 * math.log(10000.0) / ROT))
    angles = jnp.arange(SEQ, dtype=jnp.float32)[:, None] * frequency[None, :]
    return (jnp.cos(angles), jnp.sin(angles))


def rotate(operand, cos_table, sine_table):
    half_rot = ROT // 2
    first_half = operand[..., :half_rot]
    second_half = operand[..., half_rot:ROT]
    cos_part = cos_table[None, :, None, :]
    sine_part = sine_table[None, :, None, :]
    return jnp.concatenate(
        [
            first_half * cos_part - second_half * sine_part,
            second_half * cos_part + first_half * sine_part,
            operand[..., ROT:],
        ],
        -1,
    )


def unrotate(operand, cos_table, sine_table):
    half_rot = ROT // 2
    first_half = operand[..., :half_rot]
    second_half = operand[..., half_rot:ROT]
    cos_part = cos_table[None, :, None, :]
    sine_part = sine_table[None, :, None, :]
    return jnp.concatenate(
        [
            first_half * cos_part + second_half * sine_part,
            second_half * cos_part - first_half * sine_part,
            operand[..., ROT:],
        ],
        -1,
    )


def block_scores(query_block, key_block, start_row, score_scale):
    scores = (
        jnp.einsum("sqhd,skhd->shqk", query_block, key_block, preferred_element_type=jnp.float32)
        * score_scale
    )
    row_ids = start_row + jnp.arange(query_block.shape[1])[:, None]
    col_ids = jnp.arange(key_block.shape[1])[None, :]
    return jnp.where(col_ids <= row_ids, scores, -1e30)


def rounded(values_in):
    return lax.optimization_barrier(values_in.astype(jnp.bfloat16)).astype(jnp.float32)


def on_device(
    layer_input,
    ln1_gain,
    ln1_bias,
    ln2_gain,
    ln2_bias,
    qkv_weight,
    qkv_bias,
    dense_weight,
    dense_bias,
    fc1_weight,
    fc1_bias,
    fc2_weight,
    fc2_bias,
    cotangent,
):
    tok_rows, model_width = layer_input.shape
    local_heads = HEADS // lax.axis_size("tensor")
    seq_count = tok_rows // SEQ
    block_rows = 512
    score_scale = HEAD_DIM ** (-0.5)
    x_float = layer_input.astype(jnp.float32)
    gain_one = ln1_gain.astype(jnp.float32)
    shift_one = ln1_bias.astype(jnp.float32)
    gain_two = ln2_gain.astype(jnp.float32)
    shift_two = ln2_bias.astype(jnp.float32)
    attn_in = normalize(x_float, gain_one, shift_one).astype(jnp.bfloat16)
    mlp_in = normalize(x_float, gain_two, shift_two).astype(jnp.bfloat16)
    qkv_all = jnp.dot(attn_in, qkv_weight, preferred_element_type=jnp.float32) + qkv_bias.astype(
        jnp.float32
    )
    qkv_all = qkv_all.reshape(seq_count, SEQ, local_heads, 3, HEAD_DIM)
    cos_table, sine_table = rotary_tables()
    queries = rotate(qkv_all[..., 0, :], cos_table, sine_table).astype(jnp.bfloat16)
    keys_rot = rotate(qkv_all[..., 1, :], cos_table, sine_table).astype(jnp.bfloat16)
    values = qkv_all[..., 2, :].astype(jnp.bfloat16)
    context_blocks = []
    log_sums = []
    for start_row in range(0, SEQ, block_rows):
        key_end = start_row + block_rows
        masked = block_scores(
            queries[:, start_row:key_end], keys_rot[:, :key_end], start_row, score_scale
        )
        row_peak = jnp.max(masked, -1, keepdims=True)
        weights = jnp.exp(masked - row_peak)
        row_total = jnp.sum(weights, -1, keepdims=True)
        probabilities = (weights / row_total).astype(jnp.bfloat16)
        log_sums.append(row_peak + jnp.log(row_total))
        context_blocks.append(
            jnp.einsum(
                "shqk,skhd->sqhd",
                probabilities,
                values[:, :key_end],
                preferred_element_type=jnp.float32,
            )
        )
    context = jnp.concatenate(context_blocks, 1).astype(jnp.bfloat16)
    context_flat = context.reshape(tok_rows, local_heads * HEAD_DIM)
    attn_part = jnp.einsum(
        "td,ed->te", context_flat, dense_weight, preferred_element_type=jnp.float32
    )
    hidden = jnp.dot(mlp_in, fc1_weight, preferred_element_type=jnp.float32) + fc1_bias.astype(
        jnp.float32
    )
    exact_gelu = partial(jax.nn.gelu, approximate=False)
    activated = exact_gelu(hidden).astype(jnp.bfloat16)
    mlp_part = jnp.einsum("tf,ef->te", activated, fc2_weight, preferred_element_type=jnp.float32)
    partial_out = attn_part + mlp_part
    bias_total = dense_bias.astype(jnp.float32) + fc2_bias.astype(jnp.float32)
    full_sum = lax.psum(partial_out, "tensor")
    output = (x_float + full_sum + bias_total).astype(jnp.bfloat16)
    out_grad = cotangent.astype(jnp.float32)
    grad_fc2 = jnp.einsum("te,tf->ef", cotangent, activated, preferred_element_type=jnp.float32)
    grad_dense = jnp.einsum(
        "te,td->ed", cotangent, context_flat, preferred_element_type=jnp.float32
    )
    out_bias_grad = jnp.sum(out_grad, 0)
    activated_grad = jnp.einsum(
        "te,ef->tf", cotangent, fc2_weight, preferred_element_type=jnp.float32
    )
    gelu_pull = jax.vjp(exact_gelu, hidden)[1]
    hidden_grad = gelu_pull(activated_grad)[0].astype(jnp.bfloat16)
    grad_fc1 = jnp.einsum("td,tf->df", mlp_in, hidden_grad, preferred_element_type=jnp.float32)
    fc1_bias_grad = jnp.sum(hidden_grad.astype(jnp.float32), 0)
    mlp_in_grad = jnp.einsum(
        "tf,df->td", hidden_grad, fc1_weight, preferred_element_type=jnp.float32
    )
    context_grad = jnp.einsum(
        "te,ed->td", cotangent, dense_weight, preferred_element_type=jnp.float32
    ).astype(jnp.bfloat16)
    context_grad = context_grad.reshape(seq_count, SEQ, local_heads, HEAD_DIM)
    key_grad = jnp.zeros((seq_count, SEQ, local_heads, HEAD_DIM), jnp.float32)
    value_grad = jnp.zeros((seq_count, SEQ, local_heads, HEAD_DIM), jnp.float32)
    query_grads = []
    for block_number, start_row in enumerate(range(0, SEQ, block_rows)):
        key_end = start_row + block_rows
        query_block = queries[:, start_row:key_end]
        masked = block_scores(query_block, keys_rot[:, :key_end], start_row, score_scale)
        probabilities = jnp.exp(masked - log_sums[block_number])
        grad_block = context_grad[:, start_row:key_end]
        value_grad = value_grad.at[:, :key_end].add(
            jnp.einsum(
                "shqk,sqhd->skhd",
                probabilities.astype(jnp.bfloat16),
                grad_block,
                preferred_element_type=jnp.float32,
            )
        )
        prob_grad = jnp.einsum(
            "sqhd,skhd->shqk", grad_block, values[:, :key_end], preferred_element_type=jnp.float32
        )
        row_delta = jnp.sum(probabilities * prob_grad, -1, keepdims=True)
        score_grad = (probabilities * (prob_grad - row_delta)).astype(jnp.bfloat16)
        query_grads.append(
            jnp.einsum(
                "shqk,skhd->sqhd",
                score_grad,
                keys_rot[:, :key_end],
                preferred_element_type=jnp.float32,
            )
            * score_scale
        )
        key_grad = key_grad.at[:, :key_end].add(
            jnp.einsum(
                "shqk,sqhd->skhd", score_grad, query_block, preferred_element_type=jnp.float32
            )
            * score_scale
        )
    query_grad = jnp.concatenate(query_grads, 1)
    query_pre = unrotate(rounded(query_grad), cos_table, sine_table).astype(jnp.bfloat16)
    key_pre = unrotate(rounded(key_grad), cos_table, sine_table).astype(jnp.bfloat16)
    value_pre = value_grad.astype(jnp.bfloat16)
    qkv_grad = jnp.stack([query_pre, key_pre, value_pre], 3).reshape(
        tok_rows, local_heads * 3 * HEAD_DIM
    )
    grad_qkv = jnp.einsum("td,tc->dc", attn_in, qkv_grad, preferred_element_type=jnp.float32)
    qkv_bias_grad = jnp.sum(qkv_grad.astype(jnp.float32), 0)
    attn_in_grad = jnp.einsum("tc,dc->td", qkv_grad, qkv_weight, preferred_element_type=jnp.float32)
    norm_one_pull = jax.vjp(normalize, x_float, gain_one, shift_one)[1]
    input_one, gain_grad_one, shift_grad_one = norm_one_pull(attn_in_grad)
    norm_two_pull = jax.vjp(normalize, x_float, gain_two, shift_two)[1]
    input_two, gain_grad_two, shift_grad_two = norm_two_pull(mlp_in_grad)
    input_part = input_one + input_two
    input_total = lax.psum(input_part, "tensor")
    input_grad = (out_grad + input_total).astype(jnp.bfloat16)
    qkv_bias_grad, fc1_bias_grad, out_bias_grad = lax.psum(
        (qkv_bias_grad, fc1_bias_grad, out_bias_grad), "dp"
    )
    gain_grad_one, shift_grad_one, gain_grad_two, shift_grad_two = lax.psum(
        (gain_grad_one, shift_grad_one, gain_grad_two, shift_grad_two), ("dp", "tensor")
    )
    grad_qkv, grad_dense, grad_fc1, grad_fc2 = (
        lax.psum_scatter(
            grad_qkv.astype(jnp.bfloat16), "dp", scatter_dimension=0, tiled=True
        ).astype(jnp.float32),
        lax.psum_scatter(
            grad_dense.astype(jnp.bfloat16), "dp", scatter_dimension=0, tiled=True
        ).astype(jnp.float32),
        lax.psum_scatter(
            grad_fc1.astype(jnp.bfloat16), "dp", scatter_dimension=0, tiled=True
        ).astype(jnp.float32),
        lax.psum_scatter(
            grad_fc2.astype(jnp.bfloat16), "dp", scatter_dimension=0, tiled=True
        ).astype(jnp.float32),
    )
    return (
        output,
        input_grad,
        gain_grad_one,
        shift_grad_one,
        gain_grad_two,
        shift_grad_two,
        grad_qkv,
        qkv_bias_grad,
        grad_dense,
        out_bias_grad,
        grad_fc1,
        fc1_bias_grad,
        grad_fc2,
        out_bias_grad,
    )


def solution(mesh):
    in_specs = (
        P("dp", None),
        P(),
        P(),
        P(),
        P(),
        P(None, "tensor"),
        P("tensor"),
        P(None, "tensor"),
        P(),
        P(None, "tensor"),
        P("tensor"),
        P(None, "tensor"),
        P(),
        P("dp", None),
    )
    out_specs = (
        P("dp", None),
        P("dp", None),
        P(),
        P(),
        P(),
        P(),
        P("dp", "tensor"),
        P("tensor"),
        P("dp", "tensor"),
        P(),
        P("dp", "tensor"),
        P("tensor"),
        P("dp", "tensor"),
        P(),
    )
    return jax.shard_map(
        fused if fits(mesh) else on_device, mesh=mesh, in_specs=in_specs, out_specs=out_specs, check_vma=False
    )
```

profile of v0, /device:TPU:0, one launch (start us, length us, event | category | flops | bytes accessed | tf_op | source)
XLA Modules:
  0.0 297.8 jit_solution(17678792672457814959)
XLA Ops:
  0.7 0.1 pad_maximum_fusion
  0.8 0.2 multiply_sine_fusion
  1.0 0.0 copy-start.2
  1.0 0.6 copy-done.2
  1.7 283.9 %layer.1 = (bf16[1024,2048]{1,0:T(8,128)(2,1)}, bf16[1024,2048]{1,0:T(8,128)(2,1)}, bf16[256,6144]{1,0:T(8,128)(2,1)}, bf16[256,6144]{1,0:T(8,128)(2,1)}, f32[8,...) custom-call(bf16[1024,2048]{1,0:T(8,128)(2,1)} %x_hbm.1, ...), custom_call_target="tpu_custom_call" | custom-call | flops 77309411328 | bytes 134217728 | tf_op jit(solution)/shard_map/layer/pallas_call | solution.py:617
  285.5 0.0 copy-start
  285.6 10.3 %finish.1 = (f32[256,2048]{1,0:T(8,128)}, f32[256,2048]{1,0:T(8,128)}, f32[256,1536]{1,0:T(8,128)}, f32[256,512]{1,0:T(8,128)}, bf16[1024,2048]{1,0:T(8,128)(2,1)}, /*index=5*/bf16[1024,2048]{1,0:T(8,128)(2,1)}) custom-call(bf16[256,6144]{1,0:T(8,128)(2,1)} %get-tuple-element.25.kept_ref, bf16[256,6144]{1,0:T(8,128)(2,1)} %get-tuple-element.26.last_ref, ...), custom_call_target="tpu_custom_call" | custom-call | flops 1572864 | bytes 29360128 | tf_op jit(solution)/shard_map/finish/pallas_call | solution.py:648
  295.9 0.0 copy-done
  295.9 0.6 slice_reduce_fusion
  296.5 0.6 fusion.3
  297.2 0.0 copy-start.1
  297.2 0.6 copy.33
  297.8 0.0 copy-done.1
  (9 shorter events, 0.0 us)
Async XLA Ops:
  1.0 0.6 copy-start.2
  285.5 10.3 %copy-start = (f32[8,2048]{1,0:T(8,128)S(1)}, f32[8,2048]{1,0:T(8,128)}, u32[]{:S(2)}) copy-start(f32[8,2048]{1,0:T(8,128)} %get-tuple-element.31) | copy-start | bytes 196612
  297.2 0.6 copy-start.1
where the time goes:
time: 299 us; the launch traced here: 298 us
  Pallas kernels  294 us (98%)
    pallas_call x1, Pallas kernels, layer_call(): pl.pallas_call(partial(layer_kernel, jobs=jobs, orders=orders, heads=head...  284 us
    pallas_call x1, Pallas kernels, finish_call(): pl.pallas_call(finish_kernel, grid=(steps,), in_specs=ins, out_specs=outs...  10.3 us

commit v1 on v0

--- a/solution.py
+++ b/solution.py
@@ -75,14 +75,14 @@
 
 def layer_kernel(
     x_hbm, c_hbm, table_in, fc1_hbm, fc2_hbm, wqkv_hbm, dense_hbm, *refs,
-    jobs, orders, heads, block=256,
+    jobs, orders, chunks, heads, block=256,
 ):
     vec_hbm, refs = refs[:VECTORS], refs[VECTORS:]
     (
-        out_hbm, grad_hbm, keep_hbm, last_hbm, small_out, r1_hbm, r2_hbm, core_hbm, y_hbm,
+        out_hbm, grad_hbm, keep_hbm, last_hbm, small_out, r1_hbm, r2_hbm, relay_hbm, core_hbm, y_hbm,
         attn_in, mlp_in, cot, act, hg, qg, ctx, mean_ref, rstd_ref, cos_ref, sin_ref, vec, raw, w1buf, w2buf,
         s1, s2, s3, k2, ld1, ldm, ld2, piece, xrow, small, small_in,
-        load_sem, send_sem, recv_sem, keep_sem,
+        load_sem, send_sem, recv_sem, keep_sem, relay_sem,
     ) = refs
     rows, width = cot.shape
     hidden = act.shape[1]
@@ -104,7 +104,7 @@
     def t_partner(bit):
         return (me, t_flip(bit))
 
-    partners = [dp_partner(k) for k in range(3)] + [t_partner(k) for k in range(2)]
+    partners = [dp_partner(k) for k in range(3)] + [t_partner(k) for k in range(2)] + [(dp_flip(1, 2), own)]
     barrier = pltpu.get_barrier_semaphore()
     for partner in partners:
         pl.semaphore_signal(barrier, inc=1, device_id=partner, device_id_type=MESH)
@@ -186,75 +186,127 @@
     s1_slots, s2_slots, s3_slots, k2_slots = Slots(s1.shape[0]), Slots(s2.shape[0]), Slots(s3.shape[0]), Slots(k2.shape[0])
     state = {}
 
+    parts_of = {"fc2": (cot, act), "fc1": (mlp_in, hg), "qkv": (attn_in, qg), "dense": (cot, ctx)}
+    starts = list(itertools.accumulate([c[2] for c in chunks], initial=0))
+
     def operands(c):
-        n_fc = hidden // CHUNK
-        n_qkv = qg.shape[1] // CHUNK
-        if c < n_fc:
-            return cot, act, c
-        if c < 2 * n_fc:
-            return mlp_in, hg, c - n_fc
-        if c < 2 * n_fc + n_qkv:
-            return attn_in, qg, c - 2 * n_fc
-        return cot, ctx, c - 2 * n_fc - n_qkv
+        kind, first, columns = chunks[c]
+        lhs, rhs = parts_of[kind]
+        return lhs, rhs.at[:, pl.ds(first, columns)], columns
+
+    def cut(ref, columns):
+        return ref if columns == CHUNK else ref.at[..., pl.ds(0, columns)]
+
+    inner = dp_bits[1] + dp_bits[2] - 2 * dp_bits[1] * dp_bits[2]
+    relayed = any(kind == "r" for kind, _ in jobs)
 
     def block_of(lhs, index):
         return lhs[:, pl.ds(pl.multiple_of(index * nb, nb), nb)]
 
     def w1(c):
-        lhs, rhs, j = operands(c)
+        lhs, rhs, columns = operands(c)
         one, two, three = orders[c]
         slot = s1_slots.take()
         base = dp_flip(one, two, three)
+        out = cut(s1.at[slot], columns)
 
         def body(n, _):
             second, third = n // 2, lax.rem(n, 2)
             index = base - second * (1 - 2 * dp_bits[two]) * (1 << two) - third * (1 - 2 * dp_bits[three]) * (1 << three)
-            s1[slot, n] = dot(block_of(lhs, index), rhs[:, j * CHUNK : (j + 1) * CHUNK], TN).astype(bf16)
+            out[n] = dot(block_of(lhs, index), rhs[...], TN).astype(bf16)
             return 0
 
         lax.fori_loop(0, 4, body, 0)
-        copy = send_copy(s1.at[slot], r1_hbm.at[c], dp_partner(one))
+        copy = send_copy(out, cut(r1_hbm.at[c], columns), dp_partner(one))
         s1_slots.give(slot, copy.wait_send)
         state[c] = copy
 
     def w2(c):
-        lhs, rhs, j = operands(c)
+        lhs, rhs, columns = operands(c)
         one, two, three = orders[c]
         state[c].wait_recv()
-        loaded = load(r1_hbm.at[c], ld1)
+        held = cut(ld1, columns)
+        loaded = load(cut(r1_hbm.at[c], columns), held)
         slot, kept = s2_slots.take(), k2_slots.take()
         loaded.wait()
 
         def part(base, n, out):
             def body(i, _):
                 index = base - i * (1 - 2 * dp_bits[three]) * (1 << three)
-                out[i] = (dot(block_of(lhs, index), rhs[:, j * CHUNK : (j + 1) * CHUNK], TN) + ld1[n + i].astype(f32)).astype(bf16)
+                out[i] = (dot(block_of(lhs, index), rhs[...], TN) + held[n + i].astype(f32)).astype(bf16)
                 return 0
 
             lax.fori_loop(0, 2, body, 0)
 
-        part(dp_flip(two, three), 0, s2.at[slot])
-        copy = send_copy(s2.at[slot], r2_hbm.at[c], dp_partner(two))
+        sent = cut(s2.at[slot], columns)
+        part(dp_flip(two, three), 0, sent)
+        copy = send_copy(sent, cut(r2_hbm.at[c], columns), dp_partner(two))
         s2_slots.give(slot, copy.wait_send)
-        part(dp_flip(three), 2, k2.at[kept])
+        part(dp_flip(three), 2, cut(k2.at[kept], columns))
         state[c] = (copy, kept)
 
     def a3(c):
+        columns = chunks[c][2]
         copy, kept = state[c]
-        three = orders[c][2]
         copy.wait_recv()
-        loaded = load(r2_hbm.at[c], ld2)
+        held, mine = cut(ld2, columns), cut(k2.at[kept], columns)
+        loaded = load(cut(r2_hbm.at[c], columns), held)
         slot = s3_slots.take()
+        sent = cut(s3.at[slot], columns)
         loaded.wait()
-        s3[slot] = (k2[kept, 0].astype(f32) + ld2[0].astype(f32)).astype(bf16)
-        columns = pl.ds(c * CHUNK, CHUNK)
-        copy = send_copy(s3.at[slot], last_hbm.at[:, columns], dp_partner(three))
-        s3_slots.give(slot, copy.wait_send)
-        k2[kept, 1] = (k2[kept, 1].astype(f32) + ld2[1].astype(f32)).astype(bf16)
-        keep = pltpu.make_async_copy(k2.at[kept, 1], keep_hbm.at[:, columns], keep_sem.at[c])
+        sent[...] = (mine[0].astype(f32) + held[0].astype(f32)).astype(bf16)
+        place = pl.ds(starts[c], columns)
+        n = next(copies)
+        to_end, to_inner = (
+            pltpu.make_async_remote_copy(
+                src_ref=sent,
+                dst_ref=dst,
+                send_sem=send_sem.at[n],
+                recv_sem=sem,
+                device_id=partner,
+                device_id_type=MESH,
+            )
+            for dst, sem, partner in (
+                (last_hbm.at[:, place], recv_sem.at[n], dp_partner(2)),
+                (relay_hbm.at[:, place], relay_sem.at[c], dp_partner(1)),
+            )
+        )
+
+        if relayed:
+
+            @pl.when(inner == 1)
+            def _():
+                to_end.start()
+
+            @pl.when(inner == 0)
+            def _():
+                to_inner.start()
+
+        else:
+            to_end.start()
+
+        s3_slots.give(slot, to_end.wait_send)
+        mine[1] = (mine[1].astype(f32) + held[1].astype(f32)).astype(bf16)
+        keep = pltpu.make_async_copy(mine.at[1], keep_hbm.at[:, place], keep_sem.at[c])
         keep.start()
         k2_slots.give(kept, keep.wait)
-        state[c] = copy
+        passed = pltpu.make_async_remote_copy(
+            src_ref=relay_hbm.at[:, place],
+            dst_ref=last_hbm.at[:, place],
+            send_sem=send_sem.at[next(copies)],
+            recv_sem=recv_sem.at[n],
+            device_id=(dp_flip(1, 2), own),
+            device_id_type=MESH,
+        )
+        state[c] = (to_end, to_inner, passed)
+
+    def relay(c):
+        _, arriving, passed = state[c]
+
+        @pl.when(inner == 1)
+        def _():
+            arriving.wait_recv()
+            passed.start()
 
     def mlp(j):
         slot = j % 2
@@ -516,13 +568,21 @@
             state["small"] = load(small, small_out)
 
     actions = dict(
-        m=mlp, h=attention, a=w1, b=w2, c=a3, i=lambda k: sum_start(k), j=sum_middle, k=sum_late, l=sum_gather, s=small_round
+        m=mlp, h=attention, a=w1, b=w2, c=a3, i=lambda k: sum_start(k), j=sum_middle, k=sum_late, l=sum_gather, r=relay, s=small_round
     )
     for kind, n in jobs:
         actions[kind](n)
 
     for c in range(len(orders)):
-        state[c].wait_recv()
+        state[c][0].wait_recv()
+
+    if relayed:
+
+        @pl.when(inner == 1)
+        def _():
+            for c in range(len(orders)):
+                state[c][2].wait_send()
+
     for k in range(2):
         local, first, second, third = state["pieces", k]
         local.wait()
@@ -538,22 +598,24 @@
 ORDER = " ".join(
     [
         "m0 a4 a0 m1",
-        "m2 a5 m3 a7",
-        "a2 h0 b4 h1",
-        "b7 a1 a10 b5",
-        "c4 i0 c7 a11",
-        "s0 s1 b2 j0",
-        "a8 c5 b1 s2",
-        "i1 c2 j1 a3",
-        "b11 a6 b10 c1",
-        "b8 k1 c11 b3",
-        "c8 c3 s3 b6",
-        "a9 c10 l1 s4",
-        "b0 s5 k0 c6",
-        "b9 c0 c9 l0",
+        "m2 m3 a6 a7",
+        "h0 b0 h1 a3",
+        "a10 a8 b7 a1",
+        "b4 c0 a5 i0",
+        "s0 c7 b8 i1",
+        "j0 c4 s1 a13",
+        "b5 c8 a9 s2",
+        "a2 b3 a12 j1",
+        "c5 b13 b9 c3",
+        "b1 s3 c13 b2",
+        "s4 c9 b6 k1",
+        "a11 b10 c2 b12",
+        "k0 c6 c1 b11",
+        "l0 s5 l1 c10",
+        "c12 c11",
     ]
 ).split()
-Z_FIRST = (0, 5, 10)
+Z_FIRST = (1, 4, 6, 10)
 
 
 def layer_call(x, c, vectors, fc1, fc2, qkv_weight, dense):
@@ -561,10 +623,20 @@
     hidden, qkv_columns, context_columns = fc1.shape[1], qkv_weight.shape[1], dense.shape[1]
     heads = qkv_columns // (3 * HEAD_DIM)
     total = 2 * hidden + qkv_columns + context_columns
-    chunks = total // CHUNK
+    chunks = []
+    for kind, columns, widths in (
+        ("fc2", hidden, ()),
+        ("fc1", hidden, ()),
+        ("qkv", qkv_columns, (CHUNK // 2, CHUNK // 2)),
+        ("dense", context_columns, (CHUNK // 2, CHUNK // 2)),
+    ):
+        at = 0
+        for size in [CHUNK] * ((columns - sum(widths)) // CHUNK) + list(widths):
+            chunks.append((kind, at, size))
+            at += size
     vectors = [v.reshape(-1, 128) for v in vectors]
     jobs = [(word[0], int(word[1:])) for word in ORDER]
-    orders = [(1, 0, 2) if n in Z_FIRST else (0, 1, 2) for n in range(chunks)]
+    orders = [(1, 0, 2) if n in Z_FIRST else (0, 1, 2) for n in range(len(chunks))]
     quarter, nb = rows // 4, width // 8
     anywhere = pl.BlockSpec(memory_space=pl.ANY)
     local = pl.BlockSpec(memory_space=pltpu.VMEM)
@@ -575,8 +647,9 @@
         shape((nb, total), bf16),
         shape((nb, total), bf16),
         shape((8, width), f32),
-        shape((chunks, 4, nb, CHUNK), bf16),
-        shape((chunks, 2, nb, CHUNK), bf16),
+        shape((len(chunks), 4, nb, CHUNK), bf16),
+        shape((len(chunks), 2, nb, CHUNK), bf16),
+        shape((nb, total), bf16),
         shape((2, width // CHUNK * 2 * quarter, CHUNK), bf16),
         shape((2, width // CHUNK, quarter, CHUNK), bf16),
     ]
@@ -608,14 +681,15 @@
         vmem((quarter, width), bf16),
         vmem((8, width), f32),
         vmem((5, 8, width), f32),
-        pltpu.SemaphoreType.DMA((88,)),
-        pltpu.SemaphoreType.DMA((56,)),
-        pltpu.SemaphoreType.DMA((56,)),
-        pltpu.SemaphoreType.DMA((chunks,)),
+        pltpu.SemaphoreType.DMA((96,)),
+        pltpu.SemaphoreType.DMA((76,)),
+        pltpu.SemaphoreType.DMA((76,)),
+        pltpu.SemaphoreType.DMA((len(chunks),)),
+        pltpu.SemaphoreType.DMA((len(chunks),)),
     ]
     flops = 6 * rows * width * (2 * hidden + qkv_columns + context_columns)
     return pl.pallas_call(
-        partial(layer_kernel, jobs=jobs, orders=orders, heads=heads),
+        partial(layer_kernel, jobs=jobs, orders=orders, chunks=chunks, heads=heads),
         in_specs=[anywhere, anywhere, local] + [anywhere] * (4 + VECTORS),
         out_specs=[anywhere] * len(outs),
         out_shape=outs,
@@ -636,7 +710,7 @@
     refs[-1][...] = grad_ref[...]
 
 
-def finish_call(kept, last, output, input_grad, sizes, steps=4):
+def finish_call(kept, last, output, input_grad, sizes, steps=2):
     nb, total = kept.shape
     rows, width = output.shape
 
@@ -651,6 +725,7 @@
         in_specs=ins,
         out_specs=outs,
         out_shape=[jax.ShapeDtypeStruct((nb, n), f32) for n in sizes] + [jax.ShapeDtypeStruct((rows, width), bf16)] * 2,
+        compiler_params=pltpu.CompilerParams(vmem_limit_bytes=VMEM_LIMIT),
         cost_estimate=pl.CostEstimate(flops=nb * total, bytes_accessed=8 * (nb * total + rows * width), transcendentals=0),
         name="finish",
     )(kept, last, output, input_grad)

time: 299 us -> 296 us (0.990)
  Pallas kernels: 294 us -> 291 us
where the time goes in v1:
time: 296 us; the launch traced here: 295 us
  Pallas kernels  291 us (98%)
    pallas_call x1, Pallas kernels, layer_call(): pl.pallas_call(partial(layer_kernel, jobs=jobs, orders=orders, chunks=chu...  281 us
    pallas_call x1, Pallas kernels, finish_call(): pl.pallas_call(finish_kernel, grid=(steps,), in_specs=ins, out_specs=outs...  10.2 us

profile of v1, /device:TPU:0, one launch (start us, length us, event | category | flops | bytes accessed | tf_op | source)
XLA Modules:
  0.0 294.9 jit_solution(5743577277141611846)
XLA Ops:
  0.7 0.1 pad_maximum_fusion
  0.8 0.2 multiply_sine_fusion
  1.0 0.0 copy-start.2
  1.0 0.6 copy-done.2
  1.7 281.2 %layer.1 = (bf16[1024,2048]{1,0:T(8,128)(2,1)}, bf16[1024,2048]{1,0:T(8,128)(2,1)}, bf16[256,6144]{1,0:T(8,128)(2,1)}, bf16[256,6144]{1,0:T(8,128)(2,1)}, f32[8,...) custom-call(bf16[1024,2048]{1,0:T(8,128)(2,1)} %x_hbm.1, ...), custom_call_target="tpu_custom_call" | custom-call | flops 77309411328 | bytes 134217728 | tf_op jit(solution)/shard_map/layer/pallas_call | solution.py:691
  282.9 0.0 copy-start
  282.9 10.2 %finish.1 = (f32[256,2048]{1,0:T(8,128)}, f32[256,2048]{1,0:T(8,128)}, f32[256,1536]{1,0:T(8,128)}, f32[256,512]{1,0:T(8,128)}, bf16[1024,2048]{1,0:T(8,128)(2,1)}, /*index=5*/bf16[1024,2048]{1,0:T(8,128)(2,1)}) custom-call(bf16[256,6144]{1,0:T(8,128)(2,1)} %get-tuple-element.25.kept_ref, bf16[256,6144]{1,0:T(8,128)(2,1)} %get-tuple-element.26.last_ref, ...), custom_call_target="tpu_custom_call" | custom-call | flops 1572864 | bytes 29360128 | tf_op jit(solution)/shard_map/finish/pallas_call | solution.py:722
  293.1 0.0 copy-done
  293.1 0.6 slice_reduce_fusion
  293.7 0.6 fusion.3
  294.3 0.0 copy-start.1
  294.3 0.6 copy.33
  294.9 0.0 copy-done.1
  (9 shorter events, 0.0 us)
Async XLA Ops:
  1.0 0.6 copy-start.2
  282.9 10.2 %copy-start = (f32[8,2048]{1,0:T(8,128)S(1)}, f32[8,2048]{1,0:T(8,128)}, u32[]{:S(2)}) copy-start(f32[8,2048]{1,0:T(8,128)} %get-tuple-element.31) | copy-start | bytes 196612
  294.3 0.6 copy-start.1
